TPU v7x, 32 devices: a whole 2x2x4 slice. The times are simulated.
32 devices in a mesh: group: 4 (over y, x), depth: 2 (over core), mp: 4 (over z).
Axes of the slice: x: 2, y: 2, z: 4, core: 2. Of those that a mesh axis runs over, the one named last changes fastest.
Arguments:
- states: bfloat16 [64, 4096], P(('group', 'depth', 'mp')), may hold values from -6 to 6
- queries: bfloat16 [64, 32, 128], P('group', 'mp'), may hold values from -6 to 6
- new_keys: bfloat16 [64, 8, 128], P('group', 'mp'), may hold values from -18 to 18
- new_values: bfloat16 [64, 8, 128], P('group', 'mp'), may hold values from -24 to 24
- text_keys: bfloat16 [64, 8, 512, 128], P('group', 'mp', 'depth'), may hold values from -6 to 6
- text_values: bfloat16 [64, 8, 512, 128], P('group', 'mp', 'depth'), may hold values from -24 to 24
- text_length: int32 [64], P('group'), may hold values from 2 to 512
- image_keys: bfloat16 [32, 8, 576, 128], P('group', 'mp'), may hold values from -6 to 6
- image_values: bfloat16 [32, 8, 576, 128], P('group', 'mp'), may hold values from -24 to 24
- image_slot: int32 [32], replicated, may hold values from 0 to 31, as said below
- block_list: int32 [4, 32], replicated, may hold values from 0 to 31, as said below
- block_count: int32 [4], replicated, may hold values from 16 to 32, as said below
- image_first: int32 [64], P('group'), may hold values from 0 to 31, as said below
- image_count: int32 [64], P('group'), may hold values from 1 to 2
- out_weight: bfloat16 [4096, 4096], P('mp'), may hold values from -0.09375 to 0.09375
- norm_gain: float32 [4096], replicated, may hold values from 0.5 to 1.5
- gate_weight: bfloat16 [4096, 14336], P(None, ('group', 'mp')), may hold values from -0.09375 to 0.09375
- up_weight: bfloat16 [4096, 14336], P(None, ('group', 'mp')), may hold values from -0.09375 to 0.09375
- down_weight: bfloat16 [14336, 4096], P(('group', 'mp')), may hold values from -0.046875 to 0.046875
Outputs:
- attention: bfloat16 [64, 32, 128], P(('group', 'depth'), 'mp')
- layer_out: bfloat16 [64, 4096], P(('group', 'depth', 'mp'))
Inputs may be any that keep to these rules, and one draw needn't show every extreme that they name: `image_slot`: a permutation. The owner group of hash k is image_slot[k] // 8. `block_list`: the hashes of one group's list are distinct. Among one group's places with the same remainder modulo 2, at most 4 belongs to any one owner group; some group has block_count 32, and there every owner group holds exactly 4 place of every remainder. `block_count`: the sum of image_count over the group's requests. The requests of a group take consecutive list places in request order: image_first is the sum of image_count over the group's earlier requests.
All inputs are finite; a program needn't handle non-finite values.
Results may differ from a plain program's by a relative error of at most 0.012.
Values may be sent and summed in bfloat16 or wider, within the bound.
A program may use at most 128 MiB of HBM per device.

v0:
```python
import math

import jax
import jax.numpy as jnp
from jax import lax
from jax.sharding import PartitionSpec as P

LOG_TWO = math.log(2.0)
MASKED_SCORE = -1e30
NORM_EPSILON = 1e-05


def merged(part, axis, combine):
    gathered = jax.tree.map(lambda a: lax.all_gather(a, axis), part)

    def take(source):
        return jax.tree.map(lambda a: lax.dynamic_index_in_dim(a, source, 0, False), gathered)

    return lax.fori_loop(
        1, lax.axis_size(axis), lambda source, state: combine(state, take(source)), take(0)
    )


def combine(first_part, second_part):
    highest = jnp.maximum(first_part[0], second_part[0])
    first_factor = jnp.exp2(first_part[0] - highest)
    second_factor = jnp.exp2(second_part[0] - highest)
    totals = first_part[1] * first_factor + second_part[1] * second_factor
    weighted = first_part[2] * first_factor[..., None] + second_part[2] * second_factor[..., None]
    return (highest, totals, weighted)


def on_device(
    states,
    queries,
    new_keys,
    new_values,
    text_keys,
    text_values,
    text_length,
    image_keys,
    image_values,
    image_slot,
    block_list,
    block_count,
    image_first,
    image_count,
    out_weight,
    norm_gain,
    gate_weight,
    up_weight,
    down_weight,
):
    groups = lax.axis_size("group")
    depths = lax.axis_size("depth")
    group_index = lax.axis_index("group")
    depth_index = lax.axis_index("depth")
    requests, head_count, head_width = queries.shape
    kv_heads = text_keys.shape[1]
    text_span = text_keys.shape[2]
    stored = image_keys.shape[0]
    listed = block_list.shape[1]
    copies = listed // (depths * groups)
    group_share = head_count // kv_heads
    scaling = 1.0 / math.sqrt(head_width)
    grouped = queries.reshape(requests, kv_heads, group_share, head_width)
    text_scores = (
        jnp.einsum("rhgd,rhpd->rhgp", grouped, text_keys, preferred_element_type=jnp.float32)
        * scaling
    )
    new_scores = (
        jnp.einsum("rhgd,rhd->rhg", grouped, new_keys, preferred_element_type=jnp.float32) * scaling
    )
    positions = depth_index * text_span + jnp.arange(text_span, dtype=jnp.int32)
    text_allowed = (positions[None, :] < text_length[:, None])[:, None, None, :]
    new_allowed = depth_index == 0
    highest = jnp.maximum(
        jnp.max(jnp.where(text_allowed, text_scores, MASKED_SCORE), axis=-1),
        jnp.where(new_allowed, new_scores, MASKED_SCORE),
    )
    levels = jnp.floor(highest / LOG_TWO)
    text_weights = jnp.where(
        text_allowed, jnp.exp(text_scores - LOG_TWO * levels[..., None]), 0.0
    ).astype(jnp.bfloat16)
    new_weights = (
        jnp.where(new_allowed, jnp.exp(new_scores - LOG_TWO * levels), 0.0)
        .astype(jnp.bfloat16)
        .astype(jnp.float32)
    )
    totals = jnp.sum(text_weights, axis=-1, dtype=jnp.float32) + new_weights
    weighted = jnp.einsum(
        "rhgp,rhpd->rhgd", text_weights, text_values, preferred_element_type=jnp.float32
    )
    weighted = weighted + new_weights[..., None] * new_values.astype(jnp.float32)[:, :, None, :]
    local_part = (levels, totals, weighted)

    def owner_table(list_row, list_count, depth):
        indices = jnp.arange(groups * copies, dtype=jnp.int32)
        places = indices * depths + depth
        hashes = jnp.take(list_row, places, axis=0)
        slot_rows = jnp.take(image_slot, hashes, axis=0)
        owners = slot_rows // stored
        within = slot_rows % stored
        active = places < list_count
        member = (
            (owners[:, None] == jnp.arange(groups, dtype=jnp.int32)[None, :]) & active[:, None]
        ).astype(jnp.int32)
        earlier = jnp.cumsum(member, axis=0) - member
        ranked = jnp.sum(earlier * member, axis=1)
        picked = member[:, :, None] * (
            ranked[:, None, None] == jnp.arange(copies, dtype=jnp.int32)[None, None, :]
        ).astype(jnp.int32)
        chosen = jnp.sum(picked * within[:, None, None], axis=0)
        placed = jnp.sum(picked * places[:, None, None], axis=0)
        present = jnp.sum(picked, axis=0) > 0
        return (chosen, placed, present)

    own_row = lax.dynamic_index_in_dim(block_list, group_index, 0, keepdims=False)
    own_count = lax.dynamic_index_in_dim(block_count, group_index, 0, keepdims=False)
    own_chosen, own_placed, own_present = owner_table(own_row, own_count, depth_index)
    finish = image_first + image_count
    in_use = (
        own_present[None]
        & (own_placed[None] >= image_first[:, None, None])
        & (own_placed[None] < finish[:, None, None])
    )
    in_use_int = in_use.astype(jnp.int32)
    every_chosen, every_placed, every_present = jax.vmap(
        lambda list_row, list_count: owner_table(list_row, list_count, depth_index)
    )(block_list, block_count)
    serve_slots = lax.dynamic_index_in_dim(every_chosen, group_index, 1, keepdims=False)
    serve_present = lax.dynamic_index_in_dim(every_present, group_index, 1, keepdims=False)
    request_numbers = jnp.arange(requests, dtype=jnp.int32)[:, None, None]
    reader = jnp.sum(in_use_int * request_numbers, axis=0)
    routed = jnp.take(queries, reader.reshape(-1), axis=0).reshape(
        groups, copies, head_count, head_width
    )
    arrived = lax.all_to_all(routed, "group", split_axis=0, concat_axis=0, tiled=True)
    arrived = arrived.reshape(groups, copies, kv_heads, group_share, head_width)
    owned_keys = jnp.take(image_keys, serve_slots, axis=0)
    owned_values = jnp.take(image_values, serve_slots, axis=0)
    owned_scores = (
        jnp.einsum("schgd,schpd->schgp", arrived, owned_keys, preferred_element_type=jnp.float32)
        * scaling
    )
    owned_allowed = serve_present[:, :, None, None, None]
    owned_high = jnp.max(jnp.where(owned_allowed, owned_scores, MASKED_SCORE), axis=-1)
    owned_levels = jnp.floor(owned_high / LOG_TWO)
    owned_weights = jnp.where(
        owned_allowed, jnp.exp(owned_scores - LOG_TWO * owned_levels[..., None]), 0.0
    ).astype(jnp.bfloat16)
    owned_totals = jnp.sum(owned_weights, axis=-1, dtype=jnp.float32)
    owned_weighted = jnp.einsum(
        "schgp,schpd->schgd", owned_weights, owned_values, preferred_element_type=jnp.float32
    )
    back_levels, back_totals, back_weighted = (
        lax.all_to_all(owned_levels, "group", split_axis=0, concat_axis=0, tiled=True),
        lax.all_to_all(owned_totals, "group", split_axis=0, concat_axis=0, tiled=True),
        lax.all_to_all(owned_weighted, "group", split_axis=0, concat_axis=0, tiled=True),
    )
    use_float = in_use.astype(jnp.float32)
    image_levels = jnp.max(
        jnp.where(in_use[:, :, :, None, None], back_levels[None], MASKED_SCORE), axis=(1, 2)
    )
    image_totals = jnp.einsum(
        "roc,ochg->rhg", use_float, back_totals, precision=lax.Precision.HIGHEST
    )
    image_weighted = jnp.einsum(
        "roc,ochgd->rhgd", use_float, back_weighted, precision=lax.Precision.HIGHEST
    )
    image_part = (image_levels, image_totals, image_weighted)
    partial_value = combine(local_part, image_part)
    merged_levels, merged_totals, merged_weighted = merged(partial_value, "depth", combine)
    attention_all = (
        (merged_weighted / merged_totals[..., None])
        .reshape(requests, head_count, head_width)
        .astype(jnp.bfloat16)
    )
    per_depth = requests // depths
    attention_half = lax.dynamic_slice_in_dim(attention_all, depth_index * per_depth, per_depth, 0)
    flattened = attention_half.reshape(per_depth, head_count * head_width)
    picked_rows = flattened
    projected = lax.psum_scatter(
        jnp.dot(picked_rows, out_weight, preferred_element_type=jnp.float32),
        "mp",
        scatter_dimension=0,
        tiled=True,
    )
    residual = states.astype(jnp.float32) + projected
    spread = jnp.mean(residual * residual, axis=-1, keepdims=True)
    normed = (residual * lax.rsqrt(spread + NORM_EPSILON) * norm_gain).astype(jnp.bfloat16)
    piece = lax.all_gather(normed, ("group", "mp"), axis=0, tiled=True)
    gate_term = jnp.dot(piece, gate_weight, preferred_element_type=jnp.float32)
    up_term = jnp.dot(piece, up_weight, preferred_element_type=jnp.float32)
    hidden = (jax.nn.silu(gate_term) * up_term).astype(jnp.bfloat16)
    picked_rows = hidden
    summed = lax.psum_scatter(
        jnp.dot(picked_rows, down_weight, preferred_element_type=jnp.float32),
        ("group", "mp"),
        scatter_dimension=0,
        tiled=True,
    )
    return (attention_half, (residual + summed).astype(jnp.bfloat16))


def solution(mesh):
    placed = (
        P(("group", "depth", "mp"), None),
        P("group", "mp", None),
        P("group", "mp", None),
        P("group", "mp", None),
        P("group", "mp", "depth", None),
        P("group", "mp", "depth", None),
        P("group"),
        P("group", "mp", None, None),
        P("group", "mp", None, None),
        P(),
        P(),
        P(),
        P("group"),
        P("group"),
        P("mp", None),
        P(),
        P(None, ("group", "mp")),
        P(None, ("group", "mp")),
        P(("group", "mp"), None),
    )
    return jax.shard_map(
        on_device,
        mesh=mesh,
        in_specs=placed,
        out_specs=(P(("group", "depth"), "mp", None), P(("group", "depth", "mp"), None)),
        check_vma=False,
    )
```

profile of v0, /device:TPU:0, one launch (start us, length us, event | category | flops | bytes accessed | tf_op | source)
XLA Modules:
  0.0 287.0 jit_solution(1384392448140040377)
XLA Ops:
  7.2 0.8 fusion.52
  8.1 0.7 gather_fusion.3
  8.8 1.3 gather_fusion.4
  10.1 1.2 dynamic_slice.43
  11.4 0.7 broadcast_compare_fusion.3
  12.2 0.2 select_reduce_fusion.5
  12.4 0.2 multiply_reduce_fusion.2
  12.7 0.1 copy.117
  12.8 0.7 add.205
  13.5 0.9 select_reduce_fusion.4
  14.4 0.1 copy.125
  14.6 1.3 gather_fusion.2
  15.9 0.7 broadcast_select_fusion
  16.6 5.2 %all-to-all-start = ((bf16[4,4,8,128]{3,2,1,0:T(8,128)(2,1)}), bf16[4,4,8,128]{3,2,1,0:T(8,128)(2,1)S(1)}, u32[]{:S(2)}, u32[]{:S(2)}) async-start(bf16[4,4,8,128]{3,2,1,0:T(8,128)(2,1)} %broadcast_select_fusion), calls=%async_computation | async-start | bytes 65536 | tf_op jit(solution)/shard_map/all_to_all | solution.py:138
  21.8 0.8 copy.120
  22.6 0.7 broadcast_compare_fusion.1
  23.3 0.6 gather_fusion
  24.1 1.4 gather_fusion.1
  26.0 0.1 copy.124
  26.1 0.2 select_reduce_fusion.3
  26.4 0.6 multiply_reduce_fusion
  27.2 0.7 broadcast_compare_fusion
  27.9 2.3 select_reduce_fusion.1
  30.3 0.1 copy.113
  30.4 0.2 fusion.36
  30.7 0.1 copy.114
  30.8 0.2 convert_reduce_fusion.1
  31.1 3.3 %gather_fusion.5 = bf16[16,2,576,128]{3,2,1,0:T(8,128)(2,1)} fusion(bf16[8,2,576,128]{3,2,1,0:T(8,128)(2,1)S(1)} %copy-done, s32[1024]{0:T(1024)S(1)} %pad_clamp_fusion), kind=kCustom, calls=%fused_computation.1.clone | custom fusion | bytes 9437248 | tf_op jit(solution)/shard_map/jit(_take)/gather | solution.py:140
  34.5 5.0 %gather_fusion.6 = bf16[16,2,576,128]{3,2,1,0:T(8,128)(2,1)} fusion(bf16[8,2,576,128]{3,2,1,0:T(8,128)(2,1)} %param.31, s32[1024]{0:T(1024)S(1)} %pad_clamp_fusion), kind=kCustom, calls=%fused_computation.3.clone | custom fusion | bytes 9437248 | tf_op jit(solution)/shard_map/jit(_take)/gather | solution.py:141
  39.4 4.0 %select_reduce_fusion = (f32[4,4,2,4]{3,2,1,0:T(2,128)S(1)}, f32[4,4,2,4,576]{4,3,2,1,0:T(4,128)S(1)}) fusion(pred[4,4]{1,0:T(4,128)(4,1)S(1)} %bitcast.98, bf16[4,4,2,4,128]{4,3,2,1,0:T(4,128)(2,1)S(1)} %bitcast.91, bf16[4,4,2,576,128]{4,3,2,1,0:T(8,128)(2,1)} %bitcast.83, pred[4,4]{1,0:T(4,128)(4,1)S(1)} %compare_and_fusion.1), kind=kOutput, calls=%fused_computation.29 | convolution fusion | flops 21454720 | bytes 5046816 | tf_op jit(solution)/shard_map/schgd,schpd->schgp/dot_general | solution.py:143
  43.4 0.6 multiply_floor_fusion
  44.0 4.2 %all-to-all-start.1 = ((f32[4,4,2,4]{3,2,1,0:T(2,128)}), f32[4,4,2,4]{3,2,1,0:T(2,128)S(1)}, u32[]{:S(2)}, u32[]{:S(2)}) async-start(f32[4,4,2,4]{3,2,1,0:T(2,128)} %get-tuple-element.49), calls=%async_computation.1 | async-start | bytes 32768 | tf_op jit(solution)/shard_map/all_to_all | solution.py:157
  48.2 3.2 %fusion = f32[4,4,2,4,128]{4,3,2,1,0:T(4,128)S(1)} fusion(bf16[4,4,2,576,128]{4,3,2,1,0:T(8,128)(2,1)} %bitcast.82, pred[4,4]{1,0:T(4,128)(4,1)S(1)} %compare_and_fusion.1, f32[4,4,2,4,576]{4,3,2,1,0:T(4,128)S(1)} %get-tuple-element.53, f32[4,4,2,4]{3,2,1,0:T(2,128)S(1)} %get-tuple-element.50, pred[4,4]{1,0:T(4,128)(4,1)S(1)} %bitcast.99), kind=kOutput, calls=%fused_computation.7 | convolution fusion | flops 21454848 | bytes 5079584 | tf_op jit(solution)/shard_map/schgp,schpd->schgd/dot_general | solution.py:153
  51.5 0.3 convert_reduce_fusion
  51.8 0.6 copy.141
  52.4 0.6 copy.131
  53.0 4.2 %all-to-all-start.3 = ((f32[4,4,2,4]{3,1,2,0:T(4,128)}), f32[4,4,2,4]{3,1,2,0:T(4,128)S(1)}, u32[]{:S(2)}, u32[]{:S(2)}) async-start(f32[4,4,2,4]{3,1,2,0:T(4,128)} %copy.141), calls=%async_computation.3 | async-start | bytes 32768 | tf_op jit(solution)/shard_map/all_to_all | solution.py:158
  57.2 0.1 select_reduce_fusion.2
  57.4 0.1 copy.135
  57.5 4.5 %all-to-all-done.3 = f32[4,4,2,4]{3,1,2,0:T(4,128)S(1)} async-done(((f32[4,4,2,4]{3,1,2,0:T(4,128)}), f32[4,4,2,4]{3,1,2,0:T(4,128)S(1)}, u32[]{:S(2)}, u32[]{:S(2)}) %all-to-all-start.3) | async-done | bytes 544 | tf_op jit(solution)/shard_map/all_to_all | solution.py:158
  62.0 3.3 %all-to-all-start.2 = ((f32[4,4,2,4,128]{4,1,3,2,0:T(4,128)}), f32[4,4,2,4,128]{4,1,3,2,0:T(4,128)S(1)}, u32[]{:S(2)}, u32[]{:S(2)}) async-start(f32[4,4,2,4,128]{4,1,3,2,0:T(4,128)} %copy.131), calls=%async_computation.2 | async-start | bytes 131072 | tf_op jit(solution)/shard_map/all_to_all | solution.py:159
  65.3 0.2 fusion.15
  65.5 0.1 copy.143
  65.6 1.8 all-gather.2
  67.6 1.8 all-gather.1
  69.9 0.1 copy.133
  70.0 0.1 copy.115
  70.0 0.1 copy.130
  70.1 0.2 convolution_bitcast_fusion
  70.4 2.0 fusion.13
  72.4 1.9 all-gather
  74.3 0.1 fusion.28
  74.5 5.2 %fusion.31 = f32[8,4096]{1,0:T(8,128)} fusion(bf16[1024,4096]{1,0:T(8,128)(2,1)} %param.37, bf16[1,8,8,128]{3,2,1,0:T(8,128)(2,1)S(1)} %bitcast.89), kind=kOutput, calls=%fused_computation.61 | convolution fusion | flops 67108864 | bytes 8536064 | tf_op jit(solution)/shard_map/dot_general | solution.py:184
  79.8 0.6 dynamic-slice
  81.1 35.1 %all-reduce.5.cloned.1.call-done = f32[8,4096]{1,0:T(8,128)} async-done(((f32[8,4096]{1,0:T(8,128)}), f32[8,4096]{1,0:T(8,128)}) %all-reduce.5.cloned.1.call-update) | async-done | bytes 131088
  116.2 1.1 multiply_reduce_fusion.1
  117.3 1.0 fusion.35
  118.3 41.7 %all-gather.3 = bf16[16,2,4096]{2,1,0:T(2,128)(2,1)S(1)} all-gather(bf16[1,2,4096]{2,1,0:T(2,128)(2,1)S(1)} %fusion.35), channel_id=1, replica_groups=mesh['group'=4,'depth'=2,'mp'=4] {'group','mp'}, dimensions={0}, use_global_device_ids=true | all-gather | bytes 278528 | tf_op jit(solution)/shard_map/all_gather | solution.py:192
  160.0 0.1 reshape.507
  160.1 4.3 %fusion.63 = f32[32,896]{1,0:T(8,128)S(1)} fusion(bf16[32,4096]{1,0:T(8,128)(2,1)S(1)} %reshape.507, bf16[4096,896]{1,0:T(8,128)(2,1)} %param.39), kind=kOutput, calls=%fused_computation.153 | convolution fusion | flops 234881024 | bytes 7716864 | tf_op jit(solution)/shard_map/dot_general | solution.py:193
  164.4 8.5 %fusion.16 = f32[32,4096]{1,0:T(8,128)} fusion(bf16[896,4096]{1,0:T(8,128)(2,1)} %param.41, bf16[32,4096]{1,0:T(8,128)(2,1)S(1)} %reshape.507, bf16[4096,896]{1,0:T(8,128)(2,1)} %param.40, f32[32,896]{1,0:T(8,128)S(1)} %fusion.63), kind=kOutput, calls=%fused_computation.26 | convolution fusion | flops 469934080 | bytes 15581184 | tf_op jit(solution)/shard_map/dot_general | solution.py:198
  172.9 0.6 dynamic-slice.2
  174.2 104.4 %all-reduce.7.cloned.1.call-done = f32[32,4096]{1,0:T(8,128)} async-done(((f32[32,4096]{1,0:T(8,128)}), f32[32,4096]{1,0:T(8,128)}) %all-reduce.7.cloned.1.call-update) | async-done | bytes 524304
  278.6 1.6 fusion.27
  (85 shorter events, 2.4 us)
Async XLA Ops:
  7.2 24.0 %copy-start = (bf16[8,2,576,128]{3,2,1,0:T(8,128)(2,1)S(1)}, bf16[8,2,576,128]{3,2,1,0:T(8,128)(2,1)}, u32[]{:S(2)}) copy-start(bf16[8,2,576,128]{3,2,1,0:T(8,128)(2,1)} %param.30) | copy-start | bytes 7077892
  7.2 23.2 %copy-start.2 = (bf16[16,8,128]{2,1,0:T(8,128)(2,1)S(1)}, bf16[16,8,128]{2,1,0:T(8,128)(2,1)}, u32[]{:S(2)}) copy-start(bf16[16,8,128]{2,1,0:T(8,128)(2,1)} %param.24) | copy-start | bytes 98308
  7.2 23.2 %copy-start.6 = (bf16[16,2,128]{2,1,0:T(2,128)(2,1)S(1)}, bf16[16,2,128]{2,1,0:T(2,128)(2,1)}, u32[]{:S(2)}) copy-start(bf16[16,2,128]{2,1,0:T(2,128)(2,1)} %param.25) | copy-start | bytes 24580
  16.6 22.8 %all-to-all-start = ((bf16[4,4,8,128]{3,2,1,0:T(8,128)(2,1)}), bf16[4,4,8,128]{3,2,1,0:T(8,128)(2,1)S(1)}, u32[]{:S(2)}, u32[]{:S(2)}) async-start(bf16[4,4,8,128]{3,2,1,0:T(8,128)(2,1)} %broadcast_select_fusion), calls=%async_computation | async-start | bytes 65536 | tf_op jit(solution)/shard_map/all_to_all | solution.py:138
  34.4 5.0 %copy-start.5 = (bf16[16,2,128]{2,1,0:T(2,128)(2,1)S(1)}, bf16[16,2,128]{2,1,0:T(2,128)(2,1)}, u32[]{:S(2)}) copy-start(bf16[16,2,128]{2,1,0:T(2,128)(2,1)} %param.26) | copy-start | bytes 24580
  44.0 9.0 %all-to-all-start.1 = ((f32[4,4,2,4]{3,2,1,0:T(2,128)}), f32[4,4,2,4]{3,2,1,0:T(2,128)S(1)}, u32[]{:S(2)}, u32[]{:S(2)}) async-start(f32[4,4,2,4]{3,2,1,0:T(2,128)} %get-tuple-element.49), calls=%async_computation.1 | async-start | bytes 32768 | tf_op jit(solution)/shard_map/all_to_all | solution.py:157
  53.0 8.9 %all-to-all-start.3 = ((f32[4,4,2,4]{3,1,2,0:T(4,128)}), f32[4,4,2,4]{3,1,2,0:T(4,128)S(1)}, u32[]{:S(2)}, u32[]{:S(2)}) async-start(f32[4,4,2,4]{3,1,2,0:T(4,128)} %copy.141), calls=%async_computation.3 | async-start | bytes 32768 | tf_op jit(solution)/shard_map/all_to_all | solution.py:158
  62.0 8.2 %all-to-all-start.2 = ((f32[4,4,2,4,128]{4,1,3,2,0:T(4,128)}), f32[4,4,2,4,128]{4,1,3,2,0:T(4,128)S(1)}, u32[]{:S(2)}, u32[]{:S(2)}) async-start(f32[4,4,2,4,128]{4,1,3,2,0:T(4,128)} %copy.131), calls=%async_computation.2 | async-start | bytes 131072 | tf_op jit(solution)/shard_map/all_to_all | solution.py:159
  65.2 51.0 %all-reduce.5.cloned.1.call-start = ((), (), s32[]{:S(2)}) async-start(), calls=%async_computation.4 | async-start | bytes 262144
  74.4 5.3 %copy-start.3 = (bf16[8,8,128]{2,1,0:T(8,128)(2,1)}, bf16[8,8,128]{2,1,0:T(8,128)(2,1)S(1)}, u32[]{:S(2)}) copy-start(bf16[8,8,128]{2,1,0:T(8,128)(2,1)S(1)} %fusion.28) | copy-start | bytes 49156
  74.5 5.3 %copy-start.8 = (u32[32]{0:T(128)S(1)}, u32[32]{0:T(128)}, u32[]{:S(2)}) copy-start(u32[32]{0:T(128)} %constant.204) | copy-start | bytes 388
  74.5 41.7 %copy-start.1 = (bf16[2,4096]{1,0:T(2,128)(2,1)S(1)}, bf16[2,4096]{1,0:T(2,128)(2,1)}, u32[]{:S(2)}) copy-start(bf16[2,4096]{1,0:T(2,128)(2,1)} %param.23) | copy-start | bytes 49156
  74.5 42.8 %copy-start.4 = (f32[4096]{0:T(1024)S(1)}, f32[4096]{0:T(1024)}, u32[]{:S(2)}) copy-start(f32[4096]{0:T(1024)} %param.38) | copy-start | bytes 49156
  79.8 198.8 %all-reduce.7.cloned.1.call-start = ((), (), s32[]{:S(2)}) async-start(), calls=%async_computation.5 | async-start | bytes 1048576
  164.4 8.6 %copy-start.7 = (u32[32]{0:T(128)S(1)}, u32[32]{0:T(128)}, u32[]{:S(2)}) copy-start(u32[32]{0:T(128)} %constant.208) | copy-start | bytes 388
Sparse Core Ops, SparseCore 0:
  79.9 36.2 all-reduce.4
  173.0 105.4 all-reduce.6
where the time goes:
time: 288 us; the launch traced here: 287 us
  waiting for transfers between devices  144 us (50%)
  blocking collectives  47.2 us (16%)
  matrix products  30.2 us (10%)
  local copies, waits for them, and re-layouts  21.6 us (8%)
  starting transfers between devices  16.9 us (6%)
  between operations  15.7 us (5%)
  other arithmetic  11.2 us (4%)
    unnamed x4, waiting for transfers between devices  140 us
    all_gather x1, blocking collectives, on_device(): piece = lax.all_gather(normed, ('group', 'mp'), axis=0, tiled=True)  41.7 us
    dot_general x1, matrix products, on_device(): jnp.dot(picked_rows, down_weight, preferred_element_type=jnp.float32)  8.51 us
  transfers between devices with their start and end apart: 6, of which 3 were waited for; matrix products, arithmetic and copies ran while one was open for 9% of the time, Pallas kernels for 0%

commit v1 on v0

v1 whole, which is shorter than its diff:
```python
import functools
import math

import jax
import jax.numpy as jnp
from jax import lax
from jax.experimental import pallas as pl
from jax.experimental.pallas import tpu as pltpu
from jax.sharding import PartitionSpec as P

LOG_TWO = math.log(2.0)
MASKED_SCORE = -1e30
NORM_EPSILON = 1e-05
READS = 2
MESH = pl.DeviceIdType.MESH
F32 = jnp.float32
BF16 = jnp.bfloat16
NT = (((1,), (1,)), ((), ()))


def tile_of(size, most):
    for tile in (most, most // 2, most // 4):
        if size % tile == 0:
            return tile
    return size


def kernel(
    dims,
    states,
    queries,
    new_keys,
    new_values,
    norm_gain,
    text_length,
    image_slot,
    block_list,
    block_count,
    image_first,
    image_count,
    text_keys_hbm,
    text_values_hbm,
    image_keys_hbm,
    image_values_hbm,
    out_weight_hbm,
    gate_hbm,
    up_hbm,
    down_hbm,
    attention_out,
    layer_out,
    text_keys,
    text_values,
    image_keys,
    image_values,
    out_weight,
    gate,
    up,
    down,
    chosen,
    codes,
    readers,
    query_send,
    query_recv,
    text_scores,
    new_scores,
    text_weights,
    text_part,
    text_recv,
    image_scores,
    image_weights,
    image_send,
    image_recv,
    merged,
    flat,
    projected,
    proj_send,
    proj_recv,
    residual,
    norm_all,
    tokens,
    tokens_low,
    gate_sum,
    up_sum,
    hidden,
    down_sum,
    down_send,
    down_recv,
    load_sem,
    query_ssem,
    query_rsem,
    text_ssem,
    text_rsem,
    image_ssem,
    image_rsem,
    proj_ssem,
    proj_rsem,
    norm_ssem,
    norm_rsem,
    down_ssem,
    down_rsem,
):
    groups, depths, mps = dims
    pieces = groups * mps
    g = lax.axis_index("group")
    d = lax.axis_index("depth")
    m = lax.axis_index("mp")
    me = g * mps + m
    requests, heads, width = queries.shape
    kv_heads, span = text_keys.shape[1], text_keys.shape[2]
    share = heads // kv_heads
    stored, patches = image_keys.shape[0], image_keys.shape[2]
    listed = block_list.shape[1]
    steps = listed // depths
    copies = listed // (depths * groups)
    per_depth = requests // depths
    rows = states.shape[0]
    model = states.shape[1]
    scaling = 1.0 / math.sqrt(width)

    pairs = (
        (text_keys_hbm, text_keys),
        (text_values_hbm, text_values),
        (image_keys_hbm, image_keys),
        (image_values_hbm, image_values),
        (out_weight_hbm, out_weight),
        (gate_hbm, gate),
        (up_hbm, up),
        (down_hbm, down),
    )
    loads = [pltpu.make_async_copy(a, b, load_sem.at[i]) for i, (a, b) in enumerate(pairs)]
    for load in loads[:5]:
        load.start()

    barrier = pltpu.get_barrier_semaphore()

    def greet_piece(k, carry):
        peer = lax.rem(me + k, pieces)
        pl.semaphore_signal(
            barrier, inc=1, device_id=(peer // mps, d, lax.rem(peer, mps)), device_id_type=MESH
        )
        return carry

    lax.fori_loop(1, pieces, greet_piece, 0)
    for e in range(1, depths):

        def greet_depth(k, carry):
            pl.semaphore_signal(
                barrier,
                inc=1,
                device_id=(lax.rem(g + k, groups), lax.rem(d + e, depths), m),
                device_id_type=MESH,
            )
            return carry

        lax.fori_loop(0, groups, greet_depth, 0)

    own_count = block_count[g]

    def place_step(i, counts):
        out = []
        for p in range(depths):
            place = i * depths + p
            owner = image_slot[block_list[g, place]] // stored
            rank = jnp.int32(0)
            for o in range(groups):
                rank = jnp.where(owner == o, counts[p * groups + o], rank)
            codes[place] = jnp.minimum(owner * copies + rank, groups * copies - 1)
            live = (place < own_count).astype(jnp.int32)
            for o in range(groups):
                out.append(counts[p * groups + o] + jnp.where(owner == o, live, 0))
        return tuple(out)

    lax.fori_loop(0, steps, place_step, (jnp.int32(0),) * (depths * groups))

    def reader_step(r, found):
        for k in range(READS):
            place = image_first[r] + k
            held = jnp.minimum(place, listed - 1)
            good = (k < image_count[r]) & (place < own_count) & (lax.rem(place, depths) == d)
            code = jnp.where(good, codes[held], -1)
            found = tuple(jnp.where(code == i, r, old) for i, old in enumerate(found))
        return found

    found = lax.fori_loop(0, requests, reader_step, (jnp.int32(0),) * (groups * copies))
    for i, reader in enumerate(found):
        readers[i] = reader
    for o in range(groups):
        for c in range(copies):
            query_send[o, c] = queries[readers[o * copies + c]]
    query_recv[g] = query_send[g]

    pl.semaphore_wait(barrier, pieces - 1 + (depths - 1) * groups)

    def query_copy(peer, slot):
        return pltpu.make_async_remote_copy(
            src_ref=query_send.at[peer],
            dst_ref=query_recv.at[slot],
            send_sem=query_ssem.at[peer],
            recv_sem=query_rsem.at[slot],
            device_id=(peer, d, m),
            device_id_type=MESH,
        )

    def over(count, action):
        def body(k, carry):
            action(k)
            return carry

        lax.fori_loop(1, count, body, 0)

    over(groups, lambda k: query_copy(lax.rem(g + k, groups), g).start())

    def serve_step(i, state):
        place = i * depths + d
        out = []
        for s in range(groups):
            rank, picked = state[s]
            slot = image_slot[block_list[s, place]]
            hit = ((slot // stored) == g) & (place < block_count[s])
            within = lax.rem(slot, stored)
            target = jnp.where(hit, rank, -1)
            picked = tuple(jnp.where(target == c, within, old) for c, old in enumerate(picked))
            out.append((rank + hit.astype(jnp.int32), picked))
        return tuple(out)

    zero = jnp.int32(0)
    served = lax.fori_loop(0, steps, serve_step, ((zero, (zero,) * copies),) * groups)
    for s in range(groups):
        for c in range(copies):
            chosen[s * copies + c] = served[s][1][c]

    def by_head(parts):
        result = parts[0]
        row = lax.broadcasted_iota(jnp.int32, result.shape, 0)
        for h in range(1, kv_heads):
            result = jnp.where(row >= h * share, parts[h], result)
        return result

    def spread_rows(small):
        return by_head(
            [jnp.broadcast_to(small[h : h + 1, :], (heads, width)) for h in range(kv_heads)]
        )

    loads[0].wait()
    lanes = lax.broadcasted_iota(jnp.int32, (heads, span), 1) + d * span

    def text_first(r, carry):
        q = queries[r]
        score = by_head(
            [
                lax.dot_general(q, text_keys[r, h], NT, preferred_element_type=F32)
                for h in range(kv_heads)
            ]
        )
        text_scores[r] = jnp.where(lanes < text_length[r], score * scaling, MASKED_SCORE)
        key = spread_rows(new_keys[r].astype(F32))
        new_score = jnp.sum(q.astype(F32) * key, axis=-1, keepdims=True) * scaling
        new_scores[r] = jnp.broadcast_to(new_score, (heads, width))
        return carry

    lax.fori_loop(0, requests, text_first, 0, unroll=4)
    is_first = jnp.full((requests, heads, width), d, jnp.int32) == 0
    score = text_scores[...]
    fresh = jnp.where(is_first, new_scores[...], MASKED_SCORE)
    top = jnp.maximum(jnp.max(score, axis=-1, keepdims=True), fresh)
    level = jnp.floor(top / LOG_TWO)
    text_part[:, 1] = level
    weight = jnp.where(
        score > 0.5 * MASKED_SCORE, jnp.exp(score - LOG_TWO * level[:, :, :1]), 0.0
    ).astype(BF16)
    text_weights[...] = weight
    fresh_weight = jnp.where(is_first, jnp.exp(new_scores[...] - LOG_TWO * level), 0.0)
    fresh_weight = fresh_weight.astype(BF16).astype(F32)
    new_scores[...] = fresh_weight
    text_part[:, 2] = jnp.sum(weight.astype(F32), axis=-1, keepdims=True) + fresh_weight
    loads[1].wait()

    def text_second(r, carry):
        w = text_weights[r]
        value = by_head(
            [
                jnp.dot(w, text_values[r, h], preferred_element_type=F32)
                for h in range(kv_heads)
            ]
        )
        text_part[r, 0] = value + new_scores[r] * spread_rows(new_values[r].astype(F32))
        return carry

    lax.fori_loop(0, requests, text_second, 0, unroll=4)

    def text_copy(peer, slot):
        return pltpu.make_async_remote_copy(
            src_ref=text_part.at[pl.ds(peer * per_depth, per_depth)],
            dst_ref=text_recv.at[slot],
            send_sem=text_ssem.at[peer],
            recv_sem=text_rsem.at[slot],
            device_id=(g, peer, m),
            device_id_type=MESH,
        )

    over(depths, lambda k: text_copy(lax.rem(d + k, depths), d).start())
    for load in loads[5:]:
        load.start()

    loads[2].wait()
    loads[3].wait()

    def serve(s):
        slots = [chosen[s * copies + c] for c in range(copies)]
        for c in range(copies):
            q = query_recv[s, c]
            image_scores[c] = scaling * by_head(
                [
                    lax.dot_general(q, image_keys[slots[c], h], NT, preferred_element_type=F32)
                    for h in range(kv_heads)
                ]
            )
        score = image_scores[...]
        level = jnp.floor(jnp.max(score, axis=-1, keepdims=True) / LOG_TWO)
        weight = jnp.exp(score - LOG_TWO * level).astype(BF16)
        image_weights[...] = weight
        total = jnp.sum(weight.astype(F32), axis=-1, keepdims=True)
        image_send[s, :, 1] = jnp.broadcast_to(level, (copies, heads, width))
        image_send[s, :, 2] = jnp.broadcast_to(total, (copies, heads, width))
        for c in range(copies):
            w = image_weights[c]
            image_send[s, c, 0] = by_head(
                [
                    jnp.dot(w, image_values[slots[c], h], preferred_element_type=F32)
                    for h in range(kv_heads)
                ]
            )

    def image_copy(peer, depth, slot, slot_depth):
        return pltpu.make_async_remote_copy(
            src_ref=image_send.at[peer],
            dst_ref=image_recv.at[slot_depth, pl.ds(slot * copies, copies)],
            send_sem=image_ssem.at[depth, peer],
            recv_sem=image_rsem.at[slot_depth, slot],
            device_id=(peer, depth, m),
            device_id_type=MESH,
        )

    serve(g)
    image_recv[d, pl.ds(g * copies, copies)] = image_send[g]
    for e in range(1, depths):
        image_copy(g, lax.rem(d + e, depths), g, d).start()

    def serve_other(k):
        s = lax.rem(g + k, groups)
        query_copy(s, s).wait_recv()
        serve(s)
        for e in range(depths):
            image_copy(s, lax.rem(d + e, depths), g, d).start()

    over(groups, serve_other)

    over(depths, lambda k: text_copy(lax.rem(d + k, depths), lax.rem(d + k, depths)).wait_recv())
    for e in range(1, depths):
        other = lax.rem(d + e, depths)
        image_copy(g, other, g, other).wait_recv()

    def image_arrival(k):
        s = lax.rem(g + k, groups)
        for e in range(depths):
            other = lax.rem(d + e, depths)
            image_copy(s, other, s, other).wait_recv()

    over(groups, image_arrival)
    text_recv[d] = text_part[pl.ds(d * per_depth, per_depth)]

    def merge(i, carry):
        r = d * per_depth + i
        parts = [tuple(text_recv[e, i, n] for n in range(3)) for e in range(depths)]
        for k in range(READS):
            place = image_first[r] + k
            good = (k < image_count[r]) & (place < own_count)
            held = jnp.minimum(place, listed - 1)
            code = codes[held]
            at = lax.rem(held, depths)
            live = jnp.full((heads, width), good.astype(jnp.int32), jnp.int32) == 1
            parts.append(
                (
                    jnp.where(live, image_recv[at, code, 0], 0.0),
                    jnp.where(live, image_recv[at, code, 1], MASKED_SCORE),
                    jnp.where(live, image_recv[at, code, 2], 0.0),
                )
            )
        highest = functools.reduce(jnp.maximum, [part[1] for part in parts])
        factors = [jnp.exp2(part[1] - highest) for part in parts]
        total = sum(part[2] * factor for part, factor in zip(parts, factors))
        value = sum(part[0] * factor for part, factor in zip(parts, factors)) / total
        merged[i] = value
        attention_out[i] = value.astype(BF16)
        return carry

    lax.fori_loop(0, per_depth, merge, 0, unroll=2)
    for h in range(heads):
        flat[:, h * width : (h + 1) * width] = merged[:, h, :]

    loads[4].wait()
    low = flat[...].astype(BF16)
    tile = tile_of(model, 512)

    def project(n, carry):
        columns = pl.ds(pl.multiple_of(n * tile, tile), tile)
        projected[:, columns] = jnp.dot(low, out_weight[:, columns], preferred_element_type=F32)
        return carry

    lax.fori_loop(0, model // tile, project, 0)
    for i in range(mps):
        proj_send[i] = projected[i * rows : (i + 1) * rows, :].astype(proj_send.dtype)

    def proj_copy(peer, slot):
        return pltpu.make_async_remote_copy(
            src_ref=proj_send.at[peer],
            dst_ref=proj_recv.at[slot],
            send_sem=proj_ssem.at[peer],
            recv_sem=proj_rsem.at[slot],
            device_id=(g, d, peer),
            device_id_type=MESH,
        )

    over(mps, lambda k: proj_copy(lax.rem(m + k, mps), m).start())
    proj_recv[m] = proj_send[m]
    over(mps, lambda k: proj_copy(lax.rem(m + k, mps), lax.rem(m + k, mps)).wait_recv())
    total = states[...].astype(F32)
    for i in range(mps):
        total = total + proj_recv[i].astype(F32)
    residual[...] = total
    spread = jnp.mean(total * total, axis=-1, keepdims=True)
    norm_all[me] = (total * lax.rsqrt(spread + NORM_EPSILON) * norm_gain[...]).astype(BF16)

    def norm_copy(peer, slot):
        return pltpu.make_async_remote_copy(
            src_ref=norm_all.at[me],
            dst_ref=norm_all.at[slot],
            send_sem=norm_ssem.at[peer],
            recv_sem=norm_rsem.at[slot],
            device_id=(peer // mps, d, lax.rem(peer, mps)),
            device_id_type=MESH,
        )

    over(pieces, lambda k: norm_copy(lax.rem(me + k, pieces), me).start())
    loads[5].wait()
    loads[6].wait()
    loads[7].wait()
    over(pieces, lambda k: norm_copy(lax.rem(me + k, pieces), lax.rem(me + k, pieces)).wait_recv())
    for i in range(pieces):
        tokens[i * rows : (i + 1) * rows, :] = norm_all[i].astype(F32)
    tokens_low[...] = tokens[...].astype(BF16)
    gate_sum[...] = jnp.zeros_like(gate_sum)
    up_sum[...] = jnp.zeros_like(up_sum)

    def expand(k, carry):
        part = pl.ds(pl.multiple_of(k * tile, tile), tile)
        x = tokens_low[:, part]
        gate_sum[...] += jnp.dot(x, gate[part, :], preferred_element_type=F32)
        up_sum[...] += jnp.dot(x, up[part, :], preferred_element_type=F32)
        return carry

    lax.fori_loop(0, model // tile, expand, 0)
    v = gate_sum[...]
    hidden[...] = (v / (1.0 + jnp.exp(-v)) * up_sum[...]).astype(BF16)

    def contract(n, carry):
        columns = pl.ds(pl.multiple_of(n * tile, tile), tile)
        down_sum[:, columns] = jnp.dot(hidden[...], down[:, columns], preferred_element_type=F32)
        return carry

    lax.fori_loop(0, model // tile, contract, 0)
    for i in range(pieces):
        down_send[i] = down_sum[i * rows : (i + 1) * rows, :].astype(down_send.dtype)

    def down_copy(peer, slot):
        return pltpu.make_async_remote_copy(
            src_ref=down_send.at[peer],
            dst_ref=down_recv.at[slot],
            send_sem=down_ssem.at[peer],
            recv_sem=down_rsem.at[slot],
            device_id=(peer // mps, d, lax.rem(peer, mps)),
            device_id_type=MESH,
        )

    over(pieces, lambda k: down_copy(lax.rem(me + k, pieces), me).start())
    down_recv[me] = down_send[me]
    over(pieces, lambda k: down_copy(lax.rem(me + k, pieces), lax.rem(me + k, pieces)).wait_recv())

    def add_piece(i, total):
        return total + down_recv[i].astype(F32)

    layer_out[...] = lax.fori_loop(0, pieces, add_piece, residual[...]).astype(BF16)

    over(groups, lambda k: query_copy(lax.rem(g + k, groups), g).wait_send())
    over(depths, lambda k: text_copy(lax.rem(d + k, depths), d).wait_send())
    for e in range(1, depths):
        image_copy(g, lax.rem(d + e, depths), g, d).wait_send()

    def image_gone(k):
        for e in range(depths):
            image_copy(lax.rem(g + k, groups), lax.rem(d + e, depths), g, d).wait_send()

    over(groups, image_gone)
    over(mps, lambda k: proj_copy(lax.rem(m + k, mps), m).wait_send())
    over(pieces, lambda k: norm_copy(lax.rem(me + k, pieces), me).wait_send())
    over(pieces, lambda k: down_copy(lax.rem(me + k, pieces), me).wait_send())


def on_device(
    states,
    queries,
    new_keys,
    new_values,
    text_keys,
    text_values,
    text_length,
    image_keys,
    image_values,
    image_slot,
    block_list,
    block_count,
    image_first,
    image_count,
    out_weight,
    norm_gain,
    gate_weight,
    up_weight,
    down_weight,
):
    groups = lax.axis_size("group")
    depths = lax.axis_size("depth")
    mps = lax.axis_size("mp")
    pieces = groups * mps
    requests, heads, width = queries.shape
    listed = block_list.shape[1]
    copies = listed // (depths * groups)
    per_depth = requests // depths
    rows, model = states.shape
    units = gate_weight.shape[1]
    span = text_keys.shape[2]
    patches = image_keys.shape[2]
    dma = pltpu.SemaphoreType.DMA
    vmem = pl.BlockSpec(memory_space=pltpu.VMEM)
    smem = pl.BlockSpec(memory_space=pltpu.SMEM)
    hbm = pl.BlockSpec(memory_space=pl.ANY)
    big = (
        text_keys,
        text_values,
        image_keys,
        image_values,
        out_weight,
        gate_weight,
        up_weight,
        down_weight,
    )
    scratch = [pltpu.VMEM(a.shape, a.dtype) for a in big]
    scratch += [
        pltpu.SMEM((groups * copies,), jnp.int32),
        pltpu.SMEM((listed,), jnp.int32),
        pltpu.SMEM((groups * copies,), jnp.int32),
        pltpu.VMEM((groups, copies, heads, width), BF16),
        pltpu.VMEM((groups, copies, heads, width), BF16),
        pltpu.VMEM((requests, heads, span), F32),
        pltpu.VMEM((requests, heads, width), F32),
        pltpu.VMEM((requests, heads, span), BF16),
        pltpu.VMEM((requests, 3, heads, width), F32),
        pltpu.VMEM((depths, per_depth, 3, heads, width), F32),
        pltpu.VMEM((copies, heads, patches), F32),
        pltpu.VMEM((copies, heads, patches), BF16),
        pltpu.VMEM((groups, copies, 3, heads, width), F32),
        pltpu.VMEM((depths, groups * copies, 3, heads, width), F32),
        pltpu.VMEM((per_depth, heads, width), F32),
        pltpu.VMEM((per_depth, heads * width), F32),
        pltpu.VMEM((per_depth, model), F32),
        pltpu.VMEM((mps, rows, model), F32),
        pltpu.VMEM((mps, rows, model), F32),
        pltpu.VMEM((rows, model), F32),
        pltpu.VMEM((pieces, rows, model), BF16),
        pltpu.VMEM((pieces * rows, model), F32),
        pltpu.VMEM((pieces * rows, model), BF16),
        pltpu.VMEM((pieces * rows, units), F32),
        pltpu.VMEM((pieces * rows, units), F32),
        pltpu.VMEM((pieces * rows, units), BF16),
        pltpu.VMEM((pieces * rows, model), F32),
        pltpu.VMEM((pieces, rows, model), BF16),
        pltpu.VMEM((pieces, rows, model), BF16),
        dma((len(big),)),
        dma((groups,)),
        dma((groups,)),
        dma((depths,)),
        dma((depths,)),
        dma((depths, groups)),
        dma((depths, groups)),
        dma((mps,)),
        dma((mps,)),
        dma((pieces,)),
        dma((pieces,)),
        dma((pieces,)),
        dma((pieces,)),
    ]
    return pl.pallas_call(
        functools.partial(kernel, (groups, depths, mps)),
        out_shape=(
            jax.ShapeDtypeStruct((per_depth, heads, width), BF16),
            jax.ShapeDtypeStruct((rows, model), BF16),
        ),
        in_specs=[vmem] * 5 + [smem] * 6 + [hbm] * 8,
        out_specs=(vmem, vmem),
        scratch_shapes=scratch,
        compiler_params=pltpu.CompilerParams(
            collective_id=0, has_side_effects=True, vmem_limit_bytes=67043328
        ),
    )(
        states,
        queries,
        new_keys,
        new_values,
        norm_gain.reshape(1, model),
        text_length,
        image_slot,
        block_list,
        block_count,
        image_first,
        image_count,
        *big,
    )


def solution(mesh):
    placed = (
        P(("group", "depth", "mp"), None),
        P("group", "mp", None),
        P("group", "mp", None),
        P("group", "mp", None),
        P("group", "mp", "depth", None),
        P("group", "mp", "depth", None),
        P("group"),
        P("group", "mp", None, None),
        P("group", "mp", None, None),
        P(),
        P(),
        P(),
        P("group"),
        P("group"),
        P("mp", None),
        P(),
        P(None, ("group", "mp")),
        P(None, ("group", "mp")),
        P(("group", "mp"), None),
    )
    return jax.shard_map(
        on_device,
        mesh=mesh,
        in_specs=placed,
        out_specs=(P(("group", "depth"), "mp", None), P(("group", "depth", "mp"), None)),
        check_vma=False,
    )
```

time: 288 us -> 50.2 us (0.17)
  waiting for transfers between devices: 144 us -> 0 us
  blocking collectives: 47.2 us -> 0 us
  Pallas kernels: 0 us -> 46.5 us
  matrix products: 30.2 us -> 0 us
  local copies, waits for them, and re-layouts: 21.6 us -> 2.66 us
  starting transfers between devices: 16.9 us -> 0 us
  between operations: 15.7 us -> 0.65 us
  other arithmetic: 11.2 us -> 0 us
    unnamed x4 -> x0, waiting for transfers between devices: 140 us -> none
    all_gather x4 -> x0, blocking collectives: 47.2 us -> none  [the longest x1 41.7 us: on_device(): piece = lax.all_gather(normed, ('group', 'mp'), axis=0, tiled=True)]
    pallas_call x0 -> x1, Pallas kernels: none -> 46.5 us  [on_device(): pl.pallas_call(functools.partial(kernel, (groups, depths, mps)), out_shap...]
    dot_general x10 -> x0, matrix products: 30.2 us -> none  [the longest x1 8.51 us: on_device(): jnp.dot(picked_rows, down_weight, preferred_element_type=jnp.float32)]
    all_to_all x4 -> x0, starting transfers between devices: 16.9 us -> none  [the longest x1 5.19 us: on_device(): lax.all_to_all(routed, 'group', split_axis=0, concat_axis=0, tiled=True)]
    gather x10 -> x0, local copies, waits for them, and re-layouts: 13.8 us -> none  [the longest x1 4.95 us: on_device(): owned_values = jnp.take(image_values, serve_slots, axis=0)]
    all_to_all x4 -> x0, waiting for transfers between devices: 4.48 us -> none  [the longest x1 4.47 us: on_device(): lax.all_to_all(owned_totals, 'group', split_axis=0, concat_axis=0, tiled=...]
    reduce_sum x8 -> x0, other arithmetic: 3.77 us -> none  [the longest x1 1.05 us: on_device(): spread = jnp.mean(residual * residual, axis=-1, keepdims=True)]
  transfers between devices with their start and end apart: 6 -> 0, of which waited for: 3 -> 0; matrix products, arithmetic and copies ran while one was open for 9% -> 0% of each run, Pallas kernels for 0% -> 0%
where the time goes in v1:
time: 50.2 us; the launch traced here: 49.8 us
  Pallas kernels  46.5 us (93%)
  local copies, waits for them, and re-layouts  2.66 us (5%)
  between operations  0.65 us (1%)
    pallas_call x1, Pallas kernels, on_device(): pl.pallas_call(functools.partial(kernel, (groups, depths, mps)), out_shap...  46.5 us
    unnamed x2, local copies, waits for them, and re-layouts  2.66 us

profile of v1, /device:TPU:0, one launch (start us, length us, event | category | flops | bytes accessed | tf_op | source)
XLA Modules:
  0.0 49.8 jit_solution(10794610880929091779)
XLA Ops:
  0.6 46.5 %shard_map.194 = (bf16[8,8,128]{2,1,0:T(8,128)(2,1)}, bf16[2,4096]{1,0:T(2,128)(2,1)}) custom-call(bf16[2,4096]{1,0:T(2,128)(2,1)} %states.1, bf16[16,8,128]{2,1,0:T(8,128)(2,1)} %queries.1, bf16[16,2,128]{2,1,0:T(2,128)(2,1)} %new_keys.1, bf16[16,2,128]{2,1,0:T(2,128)(2,1)} %new_values.1, f32[1,4096]{1,0:T(1,128)} %bitcast.1, s32[16]{0:T(128)} %text_length.1, ...), custom_call_target="tpu_custom_call" | custom-call | tf_op jit(solution)/shard_map/pallas_call | solution.py:601
  47.2 1.3 %copy.23 = bf16[8,8,128]{2,1,0:T(8,128)(2,1)} copy(bf16[8,8,128]{2,1,0:T(8,128)(2,1)} %get-tuple-element.4) | data formatting | bytes 32768
  48.5 1.3 %copy.24 = bf16[2,4096]{1,0:T(2,128)(2,1)} copy(bf16[2,4096]{1,0:T(2,128)(2,1)} %get-tuple-element.5) | data formatting | bytes 32768

commit v2 on v1

--- a/solution.py
+++ b/solution.py
@@ -69,7 +69,9 @@
     image_scores,
     image_weights,
     image_send,
+    stat_send,
     image_recv,
+    stat_recv,
     merged,
     flat,
     projected,
@@ -92,6 +94,8 @@
     text_rsem,
     image_ssem,
     image_rsem,
+    stat_ssem,
+    stat_rsem,
     proj_ssem,
     proj_rsem,
     norm_ssem,
@@ -128,7 +132,7 @@
         (down_hbm, down),
     )
     loads = [pltpu.make_async_copy(a, b, load_sem.at[i]) for i, (a, b) in enumerate(pairs)]
-    for load in loads[:5]:
+    for load in loads[:4]:
         load.start()
 
     barrier = pltpu.get_barrier_semaphore()
@@ -206,7 +210,7 @@
             action(k)
             return carry
 
-        lax.fori_loop(1, count, body, 0)
+        lax.fori_loop(1, count, body, 0, unroll=True)
 
     over(groups, lambda k: query_copy(lax.rem(g + k, groups), g).start())
 
@@ -242,6 +246,7 @@
         )
 
     loads[0].wait()
+    loads[4].start()
     lanes = lax.broadcasted_iota(jnp.int32, (heads, span), 1) + d * span
 
     def text_first(r, carry):
@@ -305,6 +310,8 @@
     loads[2].wait()
     loads[3].wait()
 
+    stat_lane = lax.broadcasted_iota(jnp.int32, (heads, width), 1)
+
     def serve(s):
         slots = [chosen[s * copies + c] for c in range(copies)]
         for c in range(copies):
@@ -320,16 +327,19 @@
         weight = jnp.exp(score - LOG_TWO * level).astype(BF16)
         image_weights[...] = weight
         total = jnp.sum(weight.astype(F32), axis=-1, keepdims=True)
-        image_send[s, :, 1] = jnp.broadcast_to(level, (copies, heads, width))
-        image_send[s, :, 2] = jnp.broadcast_to(total, (copies, heads, width))
+        stats = jnp.zeros((heads, width), F32)
+        for c in range(copies):
+            stats = jnp.where(stat_lane == 2 * c, level[c], stats)
+            stats = jnp.where(stat_lane == 2 * c + 1, total[c], stats)
+        stat_send[s] = stats
         for c in range(copies):
             w = image_weights[c]
-            image_send[s, c, 0] = by_head(
+            image_send[s, c] = by_head(
                 [
                     jnp.dot(w, image_values[slots[c], h], preferred_element_type=F32)
                     for h in range(kv_heads)
                 ]
-            )
+            ).astype(BF16)
 
     def image_copy(peer, depth, slot, slot_depth):
         return pltpu.make_async_remote_copy(
@@ -341,10 +351,22 @@
             device_id_type=MESH,
         )
 
+    def stat_copy(peer, depth, slot, slot_depth):
+        return pltpu.make_async_remote_copy(
+            src_ref=stat_send.at[peer],
+            dst_ref=stat_recv.at[slot_depth, slot],
+            send_sem=stat_ssem.at[depth, peer],
+            recv_sem=stat_rsem.at[slot_depth, slot],
+            device_id=(peer, depth, m),
+            device_id_type=MESH,
+        )
+
     serve(g)
+    stat_recv[d, g] = stat_send[g]
     image_recv[d, pl.ds(g * copies, copies)] = image_send[g]
     for e in range(1, depths):
         image_copy(g, lax.rem(d + e, depths), g, d).start()
+        stat_copy(g, lax.rem(d + e, depths), g, d).start()
 
     def serve_other(k):
         s = lax.rem(g + k, groups)
@@ -352,6 +374,7 @@
         serve(s)
         for e in range(depths):
             image_copy(s, lax.rem(d + e, depths), g, d).start()
+            stat_copy(s, lax.rem(d + e, depths), g, d).start()
 
     over(groups, serve_other)
 
@@ -359,15 +382,21 @@
     for e in range(1, depths):
         other = lax.rem(d + e, depths)
         image_copy(g, other, g, other).wait_recv()
+        stat_copy(g, other, g, other).wait_recv()
 
     def image_arrival(k):
         s = lax.rem(g + k, groups)
         for e in range(depths):
             other = lax.rem(d + e, depths)
             image_copy(s, other, s, other).wait_recv()
+            stat_copy(s, other, s, other).wait_recv()
 
     over(groups, image_arrival)
     text_recv[d] = text_part[pl.ds(d * per_depth, per_depth)]
+
+    def stat_of(stats, lane):
+        picked = jnp.sum(jnp.where(stat_lane == lane, stats, 0.0), axis=-1, keepdims=True)
+        return jnp.broadcast_to(picked, (heads, width))
 
     def merge(i, carry):
         r = d * per_depth + i
@@ -378,12 +407,14 @@
             held = jnp.minimum(place, listed - 1)
             code = codes[held]
             at = lax.rem(held, depths)
+            stats = stat_recv[at, code // copies]
+            rank = lax.rem(code, copies)
             live = jnp.full((heads, width), good.astype(jnp.int32), jnp.int32) == 1
             parts.append(
                 (
-                    jnp.where(live, image_recv[at, code, 0], 0.0),
-                    jnp.where(live, image_recv[at, code, 1], MASKED_SCORE),
-                    jnp.where(live, image_recv[at, code, 2], 0.0),
+                    jnp.where(live, image_recv[at, code].astype(F32), 0.0),
+                    jnp.where(live, stat_of(stats, 2 * rank), MASKED_SCORE),
+                    jnp.where(live, stat_of(stats, 2 * rank + 1), 0.0),
                 )
             )
         highest = functools.reduce(jnp.maximum, [part[1] for part in parts])
@@ -495,10 +526,12 @@
     over(depths, lambda k: text_copy(lax.rem(d + k, depths), d).wait_send())
     for e in range(1, depths):
         image_copy(g, lax.rem(d + e, depths), g, d).wait_send()
+        stat_copy(g, lax.rem(d + e, depths), g, d).wait_send()
 
     def image_gone(k):
         for e in range(depths):
             image_copy(lax.rem(g + k, groups), lax.rem(d + e, depths), g, d).wait_send()
+            stat_copy(lax.rem(g + k, groups), lax.rem(d + e, depths), g, d).wait_send()
 
     over(groups, image_gone)
     over(mps, lambda k: proj_copy(lax.rem(m + k, mps), m).wait_send())
@@ -567,13 +600,15 @@
         pltpu.VMEM((depths, per_depth, 3, heads, width), F32),
         pltpu.VMEM((copies, heads, patches), F32),
         pltpu.VMEM((copies, heads, patches), BF16),
-        pltpu.VMEM((groups, copies, 3, heads, width), F32),
-        pltpu.VMEM((depths, groups * copies, 3, heads, width), F32),
+        pltpu.VMEM((groups, copies, heads, width), BF16),
+        pltpu.VMEM((groups, heads, width), F32),
+        pltpu.VMEM((depths, groups * copies, heads, width), BF16),
+        pltpu.VMEM((depths, groups, heads, width), F32),
         pltpu.VMEM((per_depth, heads, width), F32),
         pltpu.VMEM((per_depth, heads * width), F32),
         pltpu.VMEM((per_depth, model), F32),
-        pltpu.VMEM((mps, rows, model), F32),
-        pltpu.VMEM((mps, rows, model), F32),
+        pltpu.VMEM((mps, rows, model), BF16),
+        pltpu.VMEM((mps, rows, model), BF16),
         pltpu.VMEM((rows, model), F32),
         pltpu.VMEM((pieces, rows, model), BF16),
         pltpu.VMEM((pieces * rows, model), F32),
@@ -589,6 +624,8 @@
         dma((groups,)),
         dma((depths,)),
         dma((depths,)),
+        dma((depths, groups)),
+        dma((depths, groups)),
         dma((depths, groups)),
         dma((depths, groups)),
         dma((mps,)),

time: 50.2 us -> 46.4 us (0.924)
  Pallas kernels: 46.5 us -> 42.7 us
    pallas_call x1, Pallas kernels: 46.5 us -> 42.7 us  [on_device(): pl.pallas_call(functools.partial(kernel, (groups, depths, mps)), out_shap...]
where the time goes in v2:
time: 46.4 us; the launch traced here: 46 us
  Pallas kernels  42.7 us (92%)
  local copies, waits for them, and re-layouts  2.66 us (6%)
  between operations  0.65 us (1%)
    pallas_call x1, Pallas kernels, on_device(): pl.pallas_call(functools.partial(kernel, (groups, depths, mps)), out_shap...  42.7 us
    unnamed x2, local copies, waits for them, and re-layouts  2.66 us

profile of v2, /device:TPU:0, one launch (start us, length us, event | category | flops | bytes accessed | tf_op | source)
XLA Modules:
  0.0 46.0 jit_solution(9792282836442375942)
XLA Ops:
  0.6 42.7 %shard_map.194 = (bf16[8,8,128]{2,1,0:T(8,128)(2,1)}, bf16[2,4096]{1,0:T(2,128)(2,1)}) custom-call(bf16[2,4096]{1,0:T(2,128)(2,1)} %states.1, bf16[16,8,128]{2,1,0:T(8,128)(2,1)} %queries.1, bf16[16,2,128]{2,1,0:T(2,128)(2,1)} %new_keys.1, bf16[16,2,128]{2,1,0:T(2,128)(2,1)} %new_values.1, f32[1,4096]{1,0:T(1,128)} %bitcast.1, s32[16]{0:T(128)} %text_length.1, ...), custom_call_target="tpu_custom_call" | custom-call | tf_op jit(solution)/shard_map/pallas_call | solution.py:638
  43.3 1.3 %copy.23 = bf16[8,8,128]{2,1,0:T(8,128)(2,1)} copy(bf16[8,8,128]{2,1,0:T(8,128)(2,1)} %get-tuple-element.4) | data formatting | bytes 32768
  44.7 1.3 %copy.24 = bf16[2,4096]{1,0:T(2,128)(2,1)} copy(bf16[2,4096]{1,0:T(2,128)(2,1)} %get-tuple-element.5) | data formatting | bytes 32768
